TPU v7x, 256 devices: a whole 4x4x8 slice. The times are simulated.
256 devices in a mesh: dp: 8 (over x, core), cls: 32 (over z, y).
Axes of the slice: x: 4, y: 4, z: 8, core: 2. Of those that a mesh axis runs over, the one named last changes fastest.
Arguments:
- centers: float32 [65536, 512], P('cls'), may hold values from -6 to 6
- momentum: float32 [65536, 512], P('cls'), may hold values from -6 to 6
- grad_rows: bfloat16 [1048576, 512], P(('dp', 'cls')), may hold values from -5400 to 5400
- row_ids: int32 [1048576], P(('dp', 'cls')), may hold values from -1 to 65535, as said below
Outputs:
- new_centers: float32 [65536, 512], P('cls')
- new_momentum: float32 [65536, 512], P('cls')
Inputs may be any that keep to these rules, and one draw needn't show every extreme that they name: `row_ids`: slots of one device come in 32 blocks of 128; block o holds only rows o * 2048 to (o + 1) * 2048 - 1 or -1; within a block the used slots come first, distinct and ascending, and one to 128 of them are used. In every draw, for some owner o, every device of some index of dp fills its whole block o.
All inputs are finite; a program needn't handle non-finite values.
Results may differ from a plain program's by a relative error of at most 0.0003.
Values may be sent and summed in bfloat16 or wider, within the bound.
A program may use at most 128 MiB of HBM per device.

v0:
```python
import math
import jax
import jax.numpy as jnp
from jax import lax
from jax.sharding import PartitionSpec as P

beta_decay = 0.9
learn_rate = 0.5
clip_rms = 1.0
eps_norm = 1e-06
eps_row = 1e-06


def padded_to(lines, peers):
    spare = -lines.shape[0] % peers
    if not spare:
        return lines
    return jnp.concatenate([lines, jnp.zeros((spare, *lines.shape[1:]), lines.dtype)])


def sum_by_parts(array, axis):
    lines = array.reshape(-1, *array.shape[1:][-1:])
    padded = padded_to(lines, lax.axis_size(axis))
    own = lax.psum_scatter(padded, axis, scatter_dimension=0, tiled=True)
    whole = lax.all_gather(own, axis, axis=0, tiled=True)
    return whole[: len(lines)].reshape(array.shape)


def from_everyone(array, axis):
    peers = lax.axis_size(axis)
    return lax.all_to_all(
        jnp.broadcast_to(array[None], (peers, *array.shape)), axis, 0, 0, tiled=True
    )


def of_everyone(array, axis):
    return from_everyone(array, axis).sum(axis=0)


def on_device(centers, momentum, grad_rows, row_ids):
    groups = lax.axis_size("cls")
    rows_dev = centers.shape[0]
    features = centers.shape[1]
    capacity = grad_rows.shape[0] // groups
    owner_of = lax.broadcasted_iota(jnp.int32, (groups, capacity), 0)
    sent_ids = row_ids.reshape(groups, capacity)
    local_ids = jnp.where(sent_ids >= 0, sent_ids - owner_of * rows_dev, -1)
    blocks = grad_rows.reshape(groups, capacity, features)
    got_rows, got_ids = (
        lax.all_to_all(blocks, "cls", split_axis=0, concat_axis=0, tiled=True),
        lax.all_to_all(local_ids, "cls", split_axis=0, concat_axis=0, tiled=True),
    )
    flat_rows = got_rows.reshape(groups * capacity, features)
    flat_ids = got_ids.reshape(groups * capacity)
    decayed = beta_decay * momentum
    onehot_rows = lax.broadcasted_iota(jnp.int32, (rows_dev, flat_ids.shape[0]), 0)
    table = (onehot_rows == flat_ids[None, :]).astype(jnp.bfloat16)
    partial_value = jnp.dot(table, flat_rows, preferred_element_type=jnp.float32)
    gradient = sum_by_parts(partial_value, "dp")
    squares = of_everyone(jnp.sum(gradient * gradient), "cls")
    ceiling = clip_rms * math.sqrt(rows_dev * groups * features)
    factor = jnp.minimum(1.0, ceiling / jnp.sqrt(squares + eps_norm))
    new_momentum = decayed + factor * gradient
    stepped = centers - learn_rate * new_momentum
    rescale = lax.rsqrt(jnp.mean(stepped * stepped, axis=1, keepdims=True) + eps_row)
    return (stepped * rescale, new_momentum)


def solution(mesh):
    placed = (P("cls", None), P("cls", None), P(("dp", "cls"), None), P(("dp", "cls")))
    return jax.shard_map(
        on_device,
        mesh=mesh,
        in_specs=placed,
        out_specs=(P("cls", None), P("cls", None)),
        check_vma=False,
    )
```

profile of v0, /device:TPU:1, one launch (start us, length us, event | category | flops | bytes accessed | tf_op | source)
XLA Modules:
  0.0 251.9 jit_solution(12827942257511966301)
XLA Ops:
  7.2 0.0 reduce-scatter.2.cloned.1.call-start
  7.2 0.8 compare_select_fusion
  8.0 20.4 %all_to_all.17 = s32[32,1,128]{2,1,0:T(1,128)S(1)} all-to-all(s32[32,1,128]{2,1,0:T(1,128)S(1)} %compare_select_fusion), channel_id=1, replica_groups=mesh['dp'=8,'cls'=32] {'cls'}, dimensions={0} | all-to-all | bytes 32768 | tf_op jit(solution)/shard_map/all_to_all | solution.py:51
  28.5 96.8 %all_to_all.18 = bf16[32,128,512]{2,1,0:T(8,128)(2,1)S(1)} all-to-all(bf16[32,128,512]{2,1,0:T(8,128)(2,1)} %bitcast.5), channel_id=1, replica_groups=mesh['dp'=8,'cls'=32] {'cls'}, dimensions={0} | all-to-all | bytes 8388608 | tf_op jit(solution)/shard_map/all_to_all | solution.py:50
  125.3 10.3 %fusion = f32[2048,512]{1,0:T(8,128)} fusion(bf16[4096,512]{1,0:T(8,128)(2,1)S(1)} %bitcast.6, s32[4096]{0:T(1024)S(1)} %bitcast.8), kind=kOutput, calls=%fused_computation.1 | convolution fusion | flops 8598323200 | bytes 8404992 | tf_op jit(solution)/shard_map/dot_general | solution.py:58
  135.6 0.0 reduce-scatter.2.cloned.1.call-update
  135.6 0.0 all-gather.2.cloned.1.call-start
  135.7 37.9 %reduce-scatter.2.cloned.1.call-done = f32[256,512]{1,0:T(8,128)} async-done(((f32[2048,512]{1,0:T(8,128)}), f32[256,512]{1,0:T(8,128)}) %reduce-scatter.2.cloned.1.call-update) | async-done | bytes 524304 | tf_op jit(solution)/shard_map/reduce_scatter | solution.py:24
  173.5 0.0 all-gather.2.cloned.1.call-update
  173.6 38.6 %all-gather.2.cloned.1.call-done = f32[2048,512]{1,0:T(8,128)} async-done(((f32[256,512]{1,0:T(8,128)}), f32[2048,512]{1,0:T(8,128)}) %all-gather.2.cloned.1.call-update) | async-done | bytes 4194320 | tf_op jit(solution)/shard_map/all_gather | solution.py:25
  212.1 3.9 %multiply_reduce_fusion.1 = f32[]{:T(128)} fusion(f32[2048,512]{1,0:T(8,128)} %all-gather.2.cloned.1.call-done), kind=kLoop, calls=%fused_computation.6 | loop fusion | flops 2097151 | bytes 4194308 | tf_op jit(solution)/shard_map/reduce_sum | solution.py:60
  216.0 0.7 broadcast_in_dim.12
  216.7 18.0 %all_to_all.19 = f32[32,1,1]{2,1,0:T(1,128)S(1)} all-to-all(f32[32,1,1]{2,1,0:T(1,128)S(1)} %broadcast_in_dim.12), channel_id=1, replica_groups=mesh['dp'=8,'cls'=32] {'cls'}, dimensions={0} | all-to-all | bytes 256 | tf_op jit(solution)/shard_map/all_to_all | solution.py:31
  234.7 0.6 reduce_sum.28
  236.0 0.0 copy-start
  236.0 5.8 %multiply_reduce_fusion = (f32[2048]{0:T(1024)S(1)}, f32[2048,512]{1,0:T(8,128)S(1)}) fusion(f32[2048,512]{1,0:T(8,128)} %param.4, f32[2048,512]{1,0:T(8,128)} %all-gather.2.cloned.1.call-done, f32[]{:T(128)S(6)} %min_shard_map.3, f32[2048,512]{1,0:T(8,128)} %param.5), kind=kLoop, calls=%fused_computation.3 | loop fusion | flops 7337984 | bytes 16785412 | tf_op jit(solution)/shard_map/reduce_sum | solution.py:65
  241.8 0.0 copy-start.1
  241.8 0.0 copy-done
  241.8 2.8 %broadcast_multiply_fusion = f32[2048,512]{1,0:T(8,128)} fusion(f32[2048]{0:T(1024)S(1)} %add_rsqrt_fusion, f32[2048,512]{1,0:T(8,128)S(1)} %copy-done, f32[2048,512]{1,0:T(8,128)S(1)} %get-tuple-element.3), kind=kLoop, calls=%fused_computation.7 | loop fusion | flops 3145728 | bytes 12591104 | tf_op jit(solution)/shard_map/mul | solution.py:66
  244.7 0.4 copy-done.1
  (2 shorter events, 0.0 us)
Async XLA Ops:
  7.2 166.4 %reduce-scatter.2.cloned.1.call-start = ((), (), s32[]{:S(2)}) async-start(), calls=%async_computation.4 | async-start | bytes 4718592 | tf_op jit(solution)/shard_map/reduce_scatter | solution.py:24
  135.6 76.5 %all-gather.2.cloned.1.call-start = ((), (), s32[]{:S(2)}) async-start(), calls=%async_computation.5 | async-start | bytes 4718592 | tf_op jit(solution)/shard_map/all_gather | solution.py:25
  236.0 5.9 %copy-start = (f32[2048,512]{1,0:T(8,128)S(1)}, f32[2048,512]{1,0:T(8,128)}, u32[]{:S(2)}) copy-start(f32[2048,512]{1,0:T(8,128)} %param.4) | copy-start | bytes 12582916
  241.8 3.3 %copy-start.1 = (f32[2048,512]{1,0:T(8,128)}, f32[2048,512]{1,0:T(8,128)S(1)}, u32[]{:S(2)}) copy-start(f32[2048,512]{1,0:T(8,128)S(1)} %get-tuple-element.3) | copy-start | bytes 12582916
Sparse Core Ops, SparseCore 0:
  135.7 37.7 reduce-scatter.1
  175.4 36.6 all-gather.1
where the time goes:
time: 252 us
  blocking collectives  135 us (54%)
  waiting for transfers between devices  76.5 us (30%)
  between operations  14.8 us (6%)
  other arithmetic  14 us (6%)
  matrix products  10.3 us (4%)
    all_to_all x1, blocking collectives, on_device(): lax.all_to_all(blocks, 'cls', split_axis=0, concat_axis=0, tiled=True)  96.8 us
    all_gather x1, waiting for transfers between devices, sum_by_parts(): whole = lax.all_gather(own, axis, axis=0, tiled=True)  38.6 us
    reduce_scatter x1, waiting for transfers between devices, sum_by_parts(): own = lax.psum_scatter(padded, axis, scatter_dimension=0, tiled=True)  37.9 us
    all_to_all x1, blocking collectives, on_device(): lax.all_to_all(local_ids, 'cls', split_axis=0, concat_axis=0, tiled=True)  20.4 us
    all_to_all x1, blocking collectives, from_everyone(): lax.all_to_all(jnp.broadcast_to(array[None], (peers, *array.shape)), axis...  18 us
    dot_general x1, matrix products, on_device(): jnp.dot(table, flat_rows, preferred_element_type=jnp.float32)  10.3 us
    reduce_sum x1, other arithmetic, on_device(): jnp.mean(stepped * stepped, axis=1, keepdims=True) + eps_row  5.82 us
  transfers between devices with their start and end apart: 2, of which 2 were waited for; matrix products, arithmetic and copies ran while one was open for 0% of the time, Pallas kernels for 0%

commit v1 on v0

--- a/solution.py
+++ b/solution.py
@@ -22,7 +22,9 @@
     lines = array.reshape(-1, *array.shape[1:][-1:])
     padded = padded_to(lines, lax.axis_size(axis))
     own = lax.psum_scatter(padded, axis, scatter_dimension=0, tiled=True)
-    whole = lax.all_gather(own, axis, axis=0, tiled=True)
+    whole = jnp.concatenate(
+        lax.all_to_all(jnp.stack([own] * lax.axis_size(axis)), axis, 0, 0), axis=0
+    )
     return whole[: len(lines)].reshape(array.shape)
 
 

time: 252 us -> 270 us (1.071)
  blocking collectives: 135 us -> 190 us
  waiting for transfers between devices: 76.5 us -> 37.9 us
  local copies, waits for them, and re-layouts: 1.09 us -> 6.52 us
  other arithmetic: 14 us -> 9.69 us
    all_to_all x0 -> x1, blocking collectives: none -> 54.5 us  [sum_by_parts(): lax.all_to_all(jnp.stack([own] * lax.axis_size(axis)), axis, 0, 0)]
    all_gather x1 -> x0, waiting for transfers between devices: 38.6 us -> none  [sum_by_parts(): whole = lax.all_gather(own, axis, axis=0, tiled=True)]
    reduce_sum x1, other arithmetic: 5.82 us -> 0.89 us  [on_device(): jnp.mean(stepped * stepped, axis=1, keepdims=True) + eps_row]
    unnamed x4 -> x8, local copies, waits for them, and re-layouts: 0.44 us -> 4.3 us
    mul x0 -> x1, other arithmetic: none -> 2.86 us  [on_device(): new_momentum = decayed + factor * gradient]
  transfers between devices with their start and end apart: 2 -> 1, of which waited for: 2 -> 1; matrix products, arithmetic and copies ran while one was open for 0% -> 0% of each run, Pallas kernels for 0% -> 0%
where the time goes in v1:
time: 270 us; the launch traced here: 269 us
  blocking collectives  190 us (70%)
  waiting for transfers between devices  37.9 us (14%)
  between operations  14.8 us (5%)
  matrix products  10.3 us (4%)
  other arithmetic  9.69 us (4%)
  local copies, waits for them, and re-layouts  6.52 us (2%)
    all_to_all x1, blocking collectives, on_device(): lax.all_to_all(blocks, 'cls', split_axis=0, concat_axis=0, tiled=True)  96.8 us
    all_to_all x1, blocking collectives, sum_by_parts(): lax.all_to_all(jnp.stack([own] * lax.axis_size(axis)), axis, 0, 0)  54.5 us
    reduce_scatter x1, waiting for transfers between devices, sum_by_parts(): own = lax.psum_scatter(padded, axis, scatter_dimension=0, tiled=True)  37.9 us
    all_to_all x1, blocking collectives, on_device(): lax.all_to_all(local_ids, 'cls', split_axis=0, concat_axis=0, tiled=True)  20.4 us
    all_to_all x1, blocking collectives, from_everyone(): lax.all_to_all(jnp.broadcast_to(array[None], (peers, *array.shape)), axis...  18.1 us
    dot_general x1, matrix products, on_device(): jnp.dot(table, flat_rows, preferred_element_type=jnp.float32)  10.3 us
  transfers between devices with their start and end apart: 1, of which 1 were waited for; matrix products, arithmetic and copies ran while one was open for 0% of the time, Pallas kernels for 0%

profile of v1, /device:TPU:1, one launch (start us, length us, event | category | flops | bytes accessed | tf_op | source)
XLA Modules:
  0.0 269.1 jit_solution(4219259355161516408)
XLA Ops:
  7.2 0.0 reduce-scatter.2.cloned.1.call-start
  7.2 0.8 compare_select_fusion
  8.0 20.4 %all_to_all.22 = s32[32,1,128]{2,1,0:T(1,128)S(1)} all-to-all(s32[32,1,128]{2,1,0:T(1,128)S(1)} %compare_select_fusion), channel_id=1, replica_groups=mesh['dp'=8,'cls'=32] {'cls'}, dimensions={0} | all-to-all | bytes 32768 | tf_op jit(solution)/shard_map/all_to_all | solution.py:53
  28.5 96.8 %all_to_all.23 = bf16[32,128,512]{2,1,0:T(8,128)(2,1)S(1)} all-to-all(bf16[32,128,512]{2,1,0:T(8,128)(2,1)} %bitcast.8), channel_id=1, replica_groups=mesh['dp'=8,'cls'=32] {'cls'}, dimensions={0} | all-to-all | bytes 8388608 | tf_op jit(solution)/shard_map/all_to_all | solution.py:52
  125.3 10.3 %fusion = f32[2048,512]{1,0:T(8,128)} fusion(bf16[4096,512]{1,0:T(8,128)(2,1)S(1)} %bitcast.9, s32[4096]{0:T(1024)S(1)} %bitcast.11), kind=kOutput, calls=%fused_computation.1 | convolution fusion | flops 8598323200 | bytes 8404992 | tf_op jit(solution)/shard_map/dot_general | solution.py:60
  135.6 0.0 reduce-scatter.2.cloned.1.call-update
  135.6 37.9 %reduce-scatter.2.cloned.1.call-done = f32[256,512]{1,0:T(8,128)} async-done(((f32[2048,512]{1,0:T(8,128)}), f32[256,512]{1,0:T(8,128)}) %reduce-scatter.2.cloned.1.call-update) | async-done | bytes 524304 | tf_op jit(solution)/shard_map/reduce_scatter | solution.py:24
  173.5 1.6 stack.2
  175.1 54.5 %all_to_all.24 = f32[8,256,512]{2,1,0:T(8,128)S(1)} all-to-all(f32[8,256,512]{2,1,0:T(8,128)S(1)} %stack.2), channel_id=1, replica_groups=mesh['dp'=8,'cls'=32] {'dp'}, dimensions={0} | all-to-all | bytes 8388608 | tf_op jit(solution)/shard_map/all_to_all | solution.py:26
  229.6 0.0 copy-start
  229.6 2.0 copy-done
  231.6 1.7 multiply_reduce_fusion.1
  233.3 0.7 broadcast_in_dim.12
  233.9 18.1 %all_to_all.25 = f32[32,1,1]{2,1,0:T(1,128)S(1)} all-to-all(f32[32,1,1]{2,1,0:T(1,128)S(1)} %broadcast_in_dim.12), channel_id=1, replica_groups=mesh['dp'=8,'cls'=32] {'cls'}, dimensions={0} | all-to-all | bytes 256 | tf_op jit(solution)/shard_map/all_to_all | solution.py:33
  252.0 0.6 reduce_sum.28
  253.4 0.0 copy-start.1
  253.4 0.0 copy-start.3
  253.4 2.9 %broadcast_multiply_fusion.1 = f32[8,256,512]{2,1,0:T(8,128)S(1)} fusion(f32[8,256,512]{2,1,0:T(8,128)} %copy-done, f32[]{:T(128)S(6)} %min_shard_map.3), kind=kLoop, calls=%fused_computation.8 | loop fusion | flops 1048576 | bytes 8388612 | tf_op jit(solution)/shard_map/mul | solution.py:65
  256.2 0.6 copy-done.1
  256.8 1.3 copy-done.3
  258.1 0.9 multiply_reduce_fusion
  259.0 0.0 copy-start.2
  259.0 2.8 %broadcast_multiply_fusion = f32[2048,512]{1,0:T(8,128)} fusion(f32[2048]{0:T(1024)S(1)} %add_rsqrt_fusion, f32[2048,512]{1,0:T(8,128)S(1)} %copy-done.1, f32[2048,512]{1,0:T(8,128)S(1)} %get-tuple-element.3), kind=kLoop, calls=%fused_computation.7 | loop fusion | flops 3145728 | bytes 12591104 | tf_op jit(solution)/shard_map/mul | solution.py:68
  261.8 0.4 copy-done.2
  (2 shorter events, 0.0 us)
Async XLA Ops:
  7.2 166.4 %reduce-scatter.2.cloned.1.call-start = ((), (), s32[]{:S(2)}) async-start(), calls=%async_computation.5 | async-start | bytes 4718592 | tf_op jit(solution)/shard_map/reduce_scatter | solution.py:24
  229.6 2.0 copy-start
  253.4 3.5 %copy-start.1 = (f32[2048,512]{1,0:T(8,128)S(1)}, f32[2048,512]{1,0:T(8,128)}, u32[]{:S(2)}) copy-start(f32[2048,512]{1,0:T(8,128)} %param.4) | copy-start | bytes 12582916
  253.4 4.7 %copy-start.3 = (f32[2048,512]{1,0:T(8,128)S(1)}, f32[2048,512]{1,0:T(8,128)}, u32[]{:S(2)}) copy-start(f32[2048,512]{1,0:T(8,128)} %param.5) | copy-start | bytes 12582916
  259.0 3.3 %copy-start.2 = (f32[2048,512]{1,0:T(8,128)}, f32[2048,512]{1,0:T(8,128)S(1)}, u32[]{:S(2)}) copy-start(f32[2048,512]{1,0:T(8,128)S(1)} %get-tuple-element.3) | copy-start | bytes 12582916
Sparse Core Ops, SparseCore 0:
  135.7 37.7 reduce-scatter.1
